TPU v7x, 512 devices: a whole 4x4x16 slice. The times are simulated.
512 devices in a mesh: blk: 512 (over x, z, y, core).
Axes of the slice: x: 4, y: 4, z: 16, core: 2. Of those that a mesh axis runs over, the one named last changes fastest.
Arguments:
- x_points: bfloat16 [16384, 128], P('blk'), may hold values from -5.2 to 5.2, as said below
- y_points: bfloat16 [16384, 128], P('blk'), may hold values from -5.2 to 5.2, as said below
Outputs:
- x_scores: float32 [16384, 3], P('blk')
- y_scores: float32 [16384, 3], P('blk')
- mmd_stat: float32 [3], replicated
- hsic_stat: float32 [3], replicated
Inputs may be any that keep to these rules, and one draw needn't show every extreme that they name: `x_points`: every entry of the first sample lies within -5.2 and 5.2. `y_points`: every entry of the second sample lies within -5.2 and 5.2.
All inputs are finite; a program needn't handle non-finite values.
Results may differ from a plain program's by a relative error of at most 0.00035.
Values may be sent and summed in bfloat16 or wider, within the bound.
A program may use at most 64 MiB of HBM per device.

v0:
```python
import jax
import jax.numpy as jnp
from jax import lax
from jax.sharding import PartitionSpec as P

WIDTHS = (0.08, 0.16, 0.32)


def folded(array, axis, dim, absorb, carry):
    whole = jax.tree.map(lambda part: lax.all_gather(part, axis, axis=dim, tiled=True), array)
    return absorb(carry, whole, jnp.int32(0))


def kernels(left, right):
    products = jnp.dot(left, right.T, preferred_element_type=jnp.float32)
    left_sq = jnp.sum(jnp.square(left.astype(jnp.float32)), axis=1)
    right_sq = jnp.sum(jnp.square(right.astype(jnp.float32)), axis=1)
    distance = jnp.maximum(left_sq[:, None] + right_sq[None, :] - 2.0 * products, 0.0)
    factor = 1.0 / (2.0 * jnp.array(WIDTHS, jnp.float32) * left.shape[1])
    return jnp.exp(-factor[:, None, None] * distance[None])


def pair_sums(left_x, left_y, right_x, right_y, offdiag):
    same_x = kernels(left_x, right_x)
    same_y = kernels(left_y, right_y)
    cross_xy = kernels(left_x, right_y)
    cross_yx = kernels(left_y, right_x)
    hadamard = same_x * same_y
    masked_x = same_x * offdiag
    masked_y = same_y * offdiag
    row_sums = jnp.stack(
        [
            jnp.sum(masked_x, 2),
            jnp.sum(masked_y, 2),
            jnp.sum(cross_xy, 2),
            jnp.sum(cross_yx, 2),
            jnp.sum(hadamard, 2),
        ]
    )
    col_sums = jnp.stack(
        [
            jnp.sum(masked_x, 1),
            jnp.sum(masked_y, 1),
            jnp.sum(cross_yx, 1),
            jnp.sum(cross_xy, 1),
            jnp.sum(hadamard, 1),
        ]
    )
    return (row_sums, col_sums)


def shards(x_points, y_points):
    local_rows = x_points.shape[0]
    own_first = lax.axis_index("blk") * local_rows
    row_index = own_first + jnp.arange(local_rows, dtype=jnp.int32)

    def add_block(running, pieces, offset):
        col_index = offset + jnp.arange(pieces[0].shape[0], dtype=jnp.int32)
        offdiag = (row_index[:, None] != col_index[None, :]).astype(jnp.float32)
        row_sums, col_sums = pair_sums(x_points, y_points, pieces[0], pieces[1], offdiag)
        return running + row_sums

    sums = folded(
        (x_points, y_points), "blk", 0, add_block, jnp.zeros((5, 3, local_rows), jnp.float32)
    )
    sum_xx, sum_yy, sum_xy, sum_yx, sum_h = (sums[0], sums[1], sums[2], sums[3], sums[4])
    full_x = sum_xx + 1.0
    full_y = sum_yy + 1.0
    partials = jnp.stack(
        [
            jnp.sum(sum_xx, 1),
            jnp.sum(sum_yy, 1),
            jnp.sum(sum_xy, 1),
            jnp.sum(sum_h, 1),
            jnp.sum(full_x * full_y, 1),
            jnp.sum(full_x, 1),
            jnp.sum(full_y, 1),
        ]
    )
    totals = lax.psum(partials, "blk")
    count_all = jnp.float32(local_rows * lax.axis_size("blk"))
    mmd_stat = count_all * (
        (totals[0] + totals[1]) / (count_all * (count_all - 1.0))
        - 2.0 * totals[2] / (count_all * count_all)
    )
    hsic_stat = (
        totals[3] - 2.0 * totals[4] / count_all + totals[5] * totals[6] / (count_all * count_all)
    ) / count_all
    x_scores = (jnp.log(sum_xx) - jnp.log(sum_xy)).T
    y_scores = (jnp.log(sum_yy) - jnp.log(sum_yx)).T
    return (x_scores, y_scores, mmd_stat, hsic_stat)


def solution(mesh):
    placed = (P("blk", None), P("blk", None))
    return jax.shard_map(
        shards,
        mesh=mesh,
        in_specs=placed,
        out_specs=(P("blk", None), P("blk", None), P(), P()),
        check_vma=False,
    )
```

profile of v0, /device:TPU:1, one launch (start us, length us, event | category | flops | bytes accessed | tf_op | source)
XLA Modules:
  0.0 544.1 jit_solution(1156685770934072207)
XLA Ops:
  7.2 0.0 all-gather.3.cloned.1.call-start
  7.2 0.7 all-gather.3.cloned.1.call-update
  7.9 0.0 all-gather.5.cloned.1.call-start
  7.9 0.7 all-gather.5.cloned.1.call-update
  8.7 0.8 multiply_reduce_fusion.4
  9.5 0.8 multiply_reduce_fusion.3
  10.3 0.2 fusion.16
  10.5 206.0 %all-gather.3.cloned.1.call-done = bf16[16384,128]{1,0:T(8,128)(2,1)} async-done(((bf16[32,128]{1,0:T(8,128)(2,1)}), bf16[16384,128]{1,0:T(8,128)(2,1)}) %all-gather.3.cloned.1.call-update) | async-done | bytes 4194320 | tf_op jit(solution)/shard_map/all_gather | solution.py:10
  216.5 3.9 multiply_reduce_fusion.1
  220.4 0.0 copy-start.2
  220.5 195.0 %all-gather.5.cloned.1.call-done = bf16[16384,128]{1,0:T(8,128)(2,1)} async-done(((bf16[32,128]{1,0:T(8,128)(2,1)}), bf16[16384,128]{1,0:T(8,128)(2,1)}) %all-gather.5.cloned.1.call-update) | async-done | bytes 4194320 | tf_op jit(solution)/shard_map/all_gather | solution.py:10
  415.5 4.1 multiply_reduce_fusion
  419.6 0.0 copy-done.2
  419.6 0.0 copy-done
  419.6 1.6 fusion.1
  421.2 0.6 copy-done.1
  421.8 1.5 fusion.3
  423.3 1.5 fusion.5
  424.9 0.0 copy-start.4
  424.9 1.6 fusion.7
  426.5 7.0 %fusion.14 = (f32[3]{0:T(128)S(1)}, f32[3,32]{1,0:T(4,128)S(1)}, f32[3]{0:T(128)S(1)}, f32[3,32]{1,0:T(4,128)S(1)}, f32[3]{0:T(128)S(1)}, /*index=5*/f32[3,32]{1,0:T(4,128)S(1)}, f32[3]{0:T(128)S(1)}, f32[3,32]{1,0:T(4,128)S(1)}) fusion(f32[32,16384]{1,0:T(8,128)S(1)} %fusion.16, f32[32,16384]{1,0:T(8,128)S(1)} %fusion.1, f32[3]{0:T(128)S(1)} %copy-done.4, ...), kind=kLoop, calls=%fused_computation.25 | loop fusion | flops 23592564 | bytes 10487356 | tf_op jit(solution)/shard_map/reduce_sum | solution.py:71
  433.5 0.7 add_reduce_fusion
  434.3 102.5 %psum.7 = f32[7,3]{1,0:T(8,128)S(1)} all-reduce(f32[7,3]{1,0:T(8,128)S(1)} %stack.31), channel_id=1, replica_groups=mesh['blk'=512] {'blk'}, use_global_device_ids=true, to_apply=%region_15.0 | all-reduce | flops 21 | bytes 168 | tf_op jit(solution)/shard_map/psum | solution.py:80
  536.8 0.5 multiply_bitcast_fusion
  (7 shorter events, 0.0 us)
Async XLA Ops:
  7.2 209.4 %all-gather.3.cloned.1.call-start = ((), (), s32[]{:S(2)}) async-start(), calls=%async_computation | async-start | bytes 4202496 | tf_op jit(solution)/shard_map/all_gather | solution.py:10
  7.9 407.6 %all-gather.5.cloned.1.call-start = ((), (), s32[]{:S(2)}) async-start(), calls=%async_computation.1 | async-start | bytes 4202496 | tf_op jit(solution)/shard_map/all_gather | solution.py:10
  220.4 199.1 %copy-start.2 = (bf16[32,128]{1,0:T(8,128)(2,1)S(1)}, bf16[32,128]{1,0:T(8,128)(2,1)}, u32[]{:S(2)}) copy-start(bf16[32,128]{1,0:T(8,128)(2,1)} %param.6) | copy-start | bytes 24580
  415.5 4.1 copy-start
  419.6 2.2 copy-start.1
  421.8 1.6 copy-start.3
  424.9 1.6 copy-start.4
Sparse Core Ops, SparseCore 0:
  12.6 203.9 all-gather.2
  221.1 194.3 all-gather.4
where the time goes:
time: 544 us
  waiting for transfers between devices  402 us (74%)
  blocking collectives  102 us (19%)
  other arithmetic  18.1 us (3%)
  between operations  14.2 us (3%)
  matrix products  6.2 us (1%)
    all_gather x2, waiting for transfers between devices, folded(): lax.all_gather(part, axis, axis=dim, tiled=True)  401 us
    psum x1, blocking collectives, shards(): totals = lax.psum(partials, 'blk')  102 us
  transfers between devices with their start and end apart: 2, of which 2 were waited for; matrix products, arithmetic and copies ran while one was open for 1% of the time, Pallas kernels for 0%

commit v1 on v0

v1 whole, which is shorter than its diff:
```python
import functools
import math

import jax
import jax.numpy as jnp
from jax import lax
from jax.experimental import pallas as pl
from jax.experimental.pallas import tpu as pltpu
from jax.sharding import PartitionSpec as P

MESH = pl.DeviceIdType.MESH
NX, NZ, NY, NC = 4, 16, 4, 2
PLANE = NX * NY * NC
PTS = 32
DIM = 128
TILES = PLANE * PTS // 128
SCALE = math.log2(math.e) / (2.0 * 0.32 * DIM)
NT = (((1,), (1,)), ((), ()))
F32 = jnp.float32
BF16 = jnp.bfloat16


def device_of(x, z, y, c):
    return ((x * NZ + z) * NY + y) * NC + c


def plane_device(q, z):
    return device_of(q // (NY * NC), z, (q // NC) % NY, q % NC)


def squares(points):
    wide = points.astype(F32)
    sq = wide * wide
    high = sq.astype(BF16)
    low = (sq - high.astype(F32)).astype(BF16)
    return high, low


def fold(tile):
    return jnp.sum(tile.reshape(-1, 8, 128), axis=0)


def powers(e):
    e2 = e * e
    return e2 * e2, e2, e


def kernel(x_hbm, y_hbm, xs_ref, ys_ref, mmd_ref, hsic_ref,
           zbuf, pbuf, rown, acc, sbuf, rbuf, tsend, trecv, usend, urecv,
           load_sem, zsend_sem, zrecv_sem, psend_sem, precv_sem, ssend_sem, srecv_sem,
           tsend_sem, trecv_sem, usend_sem, urecv_sem):
    me = lax.axis_index("blk")
    c = me % NC
    y = (me // NC) % NY
    z = (me // (NC * NY)) % NZ
    x = me // (NC * NY * NZ)
    q = (x * NY + y) * NC + c

    loads = []
    for n, (buf, slot) in enumerate(((zbuf, z), (pbuf, q))):
        for k, src in enumerate((x_hbm, y_hbm)):
            cp = pltpu.make_async_copy(src, buf.at[slot, pl.ds(PTS * k, PTS)], load_sem.at[2 * n + k])
            cp.start()
            loads.append(cp)

    barrier = pltpu.get_barrier_semaphore()

    def greet_z(d, carry):
        pl.semaphore_signal(barrier, inc=1, device_id=(device_of(x, (z + d) % NZ, y, c),), device_id_type=MESH)
        return carry

    def greet_p(d, carry):
        pl.semaphore_signal(barrier, inc=1, device_id=(plane_device((q + d) % PLANE, z),), device_id_type=MESH)
        return carry

    lax.fori_loop(1, NZ, greet_z, 0)
    lax.fori_loop(1, PLANE, greet_p, 0)
    for cp in loads:
        cp.wait()
    pl.semaphore_wait(barrier, NZ + PLANE - 2)

    def offset(d):
        return jnp.where(d % 2 == 1, (d + 1) // 2, NZ - d // 2)

    def send_z(d, carry):
        to = (z + offset(d)) % NZ
        pltpu.make_async_remote_copy(
            src_ref=zbuf.at[z], dst_ref=zbuf.at[z], send_sem=zsend_sem, recv_sem=zrecv_sem.at[z],
            device_id=(device_of(x, to, y, c),), device_id_type=MESH).start()
        return carry

    def send_p(d, carry):
        pltpu.make_async_remote_copy(
            src_ref=zbuf.at[z], dst_ref=pbuf.at[q], send_sem=psend_sem, recv_sem=precv_sem,
            device_id=(plane_device((q + d) % PLANE, z),), device_id_type=MESH).start()
        return carry

    lax.fori_loop(0, NZ - 1, lambda i, carry: send_z(NZ - 1 - i, carry), 0)
    lax.fori_loop(1, PLANE, send_p, 0)

    def wait_bytes(ref, sem):
        pltpu.make_async_copy(ref, ref, sem).wait()

    wait_bytes(pbuf.at[pl.ds(0, PLANE - 1)], precv_sem)

    acc[...] = jnp.zeros_like(acc)
    ones8 = jnp.ones((8, DIM), BF16)
    for g in range(TILES):
        for k in range(2):
            pts = pbuf[4 * g:4 * g + 4, PTS * k:PTS * k + PTS, :].reshape(128, DIM)
            high, low = squares(pts)
            norm = lax.dot_general(ones8, high, NT, preferred_element_type=F32)
            norm += lax.dot_general(ones8, low, NT, preferred_element_type=F32)
            rown[g, k] = norm * -SCALE

    def block(zi, diagonal):
        cols = zbuf[zi]
        high, low = squares(cols)
        ones = jnp.ones((DIM, 128), BF16)
        coln = jnp.dot(high, ones, preferred_element_type=F32) + jnp.dot(low, ones, preferred_element_type=F32)
        coln = coln * -SCALE
        for g in range(TILES):
            rows_x = pbuf[4 * g:4 * g + 4, 0:PTS, :].reshape(128, DIM)
            rows_y = pbuf[4 * g:4 * g + 4, PTS:2 * PTS, :].reshape(128, DIM)
            prod_x = lax.dot_general(cols, rows_x, NT, preferred_element_type=F32)
            prod_y = lax.dot_general(cols, rows_y, NT, preferred_element_type=F32)

            def gauss(prod, k, row):
                arg = prod * (2.0 * SCALE) + coln[PTS * k:PTS * k + PTS]
                arg = (arg.reshape(-1, 8, 128) + rown[g, row][None]).reshape(PTS, 128)
                return powers(jnp.exp2(jnp.minimum(arg, 0.0)))

            xx = gauss(prod_x[:PTS], 0, 0)
            xy = gauss(prod_x[PTS:], 1, 0)
            yx = gauss(prod_y[:PTS], 0, 1)
            yy = gauss(prod_y[PTS:], 1, 1)
            hh = [a * b for a, b in zip(xx, yy)]
            if diagonal:
                lane = lax.broadcasted_iota(jnp.int32, (PTS, 128), 1) + 128 * g
                sub = lax.broadcasted_iota(jnp.int32, (PTS, 128), 0) + PTS * q
                off = lane != sub
                xx = [jnp.where(off, a, 0.0) for a in xx]
                yy = [jnp.where(off, a, 0.0) for a in yy]
            for t, stat in enumerate((xx, yy, xy, yx, hh)):
                for b in range(3):
                    acc[g, t * 3 + b] += fold(stat[b])

    block(z, True)

    def step(d, carry):
        zi = (z + offset(d)) % NZ
        pltpu.make_async_copy(zbuf.at[zi], zbuf.at[zi], zrecv_sem.at[zi]).wait()
        block(zi, False)
        return carry

    lax.fori_loop(1, NZ, step, 0)

    for g in range(TILES):
        def row(t, b):
            return jnp.sum(acc[g, t * 3 + b], axis=0, keepdims=True)
        zero = jnp.zeros((1, 128), F32)
        groups = [jnp.concatenate([row(k, 0), row(k, 1), row(k, 2), row(4, k) if k < 3 else zero], axis=0) for k in range(4)]
        for m in range(4):
            sbuf[4 * g + m] = jnp.concatenate([groups[k][:, PTS * m:PTS * m + PTS] for k in range(4)], axis=1)

    def send_s(d, carry):
        to = (q + d) % PLANE
        pltpu.make_async_remote_copy(
            src_ref=sbuf.at[to], dst_ref=rbuf.at[q], send_sem=ssend_sem, recv_sem=srecv_sem,
            device_id=(plane_device(to, z),), device_id_type=MESH).start()
        return carry

    lax.fori_loop(1, PLANE, send_s, 0)
    rbuf[q] = sbuf[q]
    wait_bytes(rbuf.at[pl.ds(0, PLANE - 1)], srecv_sem)
    sums = jnp.sum(rbuf[...], axis=0)
    full = sums + 1.0
    prod = full * pltpu.roll(full, 128 - PTS, 1)
    lane = lax.broadcasted_iota(jnp.int32, (4, 128), 1)
    sub = lax.broadcasted_iota(jnp.int32, (4, 128), 0)
    packed = jnp.zeros((4, 128), F32)
    for k in range(5):
        src = prod if k == 4 else sums
        lo = PTS * (k % 4)
        tot = jnp.sum(jnp.where((lane >= lo) & (lane < lo + PTS), src, 0.0), axis=1, keepdims=True)
        packed = jnp.where(lane == 8 * sub + k, tot, packed)
    tsend[...] = jnp.sum(packed, axis=0, keepdims=True)

    def send_t(d, carry):
        pltpu.make_async_remote_copy(
            src_ref=tsend, dst_ref=trecv.at[q], send_sem=tsend_sem, recv_sem=trecv_sem,
            device_id=(plane_device((q + d) % PLANE, z),), device_id_type=MESH).start()
        return carry

    lax.fori_loop(1, PLANE, send_t, 0)
    trecv[q] = tsend[...]

    logs = jnp.log(sums)
    score = logs - pltpu.roll(logs, 64, 1)
    score = jnp.concatenate([score, score], axis=0)
    turned = jnp.transpose(jnp.concatenate([score] * 16, axis=0))
    xs_ref[...] = turned[0:PTS, 0:3]
    ys_ref[...] = turned[PTS:2 * PTS, 0:3]

    wait_bytes(trecv.at[pl.ds(0, PLANE - 1)], trecv_sem)
    usend[...] = jnp.sum(trecv[...], axis=0)

    def send_u(d, carry):
        pltpu.make_async_remote_copy(
            src_ref=usend, dst_ref=urecv.at[z], send_sem=usend_sem, recv_sem=urecv_sem,
            device_id=(device_of(x, (z + d) % NZ, y, c),), device_id_type=MESH).start()
        return carry

    lax.fori_loop(1, NZ, send_u, 0)
    urecv[z] = usend[...]
    wait_bytes(urecv.at[pl.ds(0, NZ - 1)], urecv_sem)
    tot = jnp.broadcast_to(jnp.sum(urecv[...], axis=0), (8, 128))

    n = float(PTS * PLANE * NZ)

    def at(k, b):
        return tot[0:1, 8 * b + k:8 * b + k + 1]

    for b in range(3):
        txx, tyy, txy, tpr = at(0, b), at(1, b), at(2, b), at(4, b)
        th = tot[0:1, 8 * 3 + b:8 * 3 + b + 1]
        mmd_ref[0:1, b:b + 1] = n * ((txx + tyy) / (n * (n - 1.0)) - 2.0 * txy / (n * n))
        hsic_ref[0:1, b:b + 1] = (th - 2.0 * tpr / n + (txx + n) * (tyy + n) / (n * n)) / n

    wait_bytes(zbuf.at[pl.ds(0, NZ - 1)], zsend_sem)
    wait_bytes(pbuf.at[pl.ds(0, PLANE - 1)], psend_sem)
    wait_bytes(sbuf.at[pl.ds(0, PLANE - 1)], ssend_sem)
    wait_bytes(trecv.at[pl.ds(0, PLANE - 1)], tsend_sem)
    wait_bytes(urecv.at[pl.ds(0, NZ - 1)], usend_sem)


def shards(x_points, y_points):
    dma = pltpu.SemaphoreType.DMA
    vmem = pl.BlockSpec(memory_space=pltpu.VMEM)
    xs, ys, mmd, hsic = pl.pallas_call(
        kernel,
        out_shape=(
            jax.ShapeDtypeStruct((PTS, 3), F32),
            jax.ShapeDtypeStruct((PTS, 3), F32),
            jax.ShapeDtypeStruct((1, 3), F32),
            jax.ShapeDtypeStruct((1, 3), F32),
        ),
        in_specs=[pl.BlockSpec(memory_space=pl.ANY)] * 2,
        out_specs=(vmem,) * 4,
        scratch_shapes=[
            pltpu.VMEM((NZ, 2 * PTS, DIM), BF16),
            pltpu.VMEM((PLANE, 2 * PTS, DIM), BF16),
            pltpu.VMEM((TILES, 2, 8, 128), F32),
            pltpu.VMEM((TILES, 15, 8, 128), F32),
            pltpu.VMEM((PLANE, 4, 128), F32),
            pltpu.VMEM((PLANE, 4, 128), F32),
            pltpu.VMEM((1, 128), F32),
            pltpu.VMEM((PLANE, 1, 128), F32),
            pltpu.VMEM((1, 128), F32),
            pltpu.VMEM((NZ, 1, 128), F32),
            dma((4,)), dma, dma((NZ,)), dma, dma, dma, dma, dma, dma, dma, dma,
        ],
        compiler_params=pltpu.CompilerParams(collective_id=0, has_side_effects=True),
        name="mmd_hsic",
    )(x_points, y_points)
    return xs, ys, mmd.reshape(3), hsic.reshape(3)


def solution(mesh):
    return jax.shard_map(
        shards,
        mesh=mesh,
        in_specs=(P("blk", None), P("blk", None)),
        out_specs=(P("blk", None), P("blk", None), P(), P()),
        check_vma=False,
    )
```

time: 544 us -> 59.1 us (0.11)
  waiting for transfers between devices: 402 us -> 0 us
  blocking collectives: 102 us -> 0 us
  Pallas kernels: 0 us -> 55.1 us
  other arithmetic: 18.1 us -> 0 us
  between operations: 14.2 us -> 0.65 us
  matrix products: 6.2 us -> 0 us
    all_gather x2 -> x0, waiting for transfers between devices: 401 us -> none  [folded(): lax.all_gather(part, axis, axis=dim, tiled=True)]
    psum x1 -> x0, blocking collectives: 102 us -> none  [shards(): totals = lax.psum(partials, 'blk')]
    pallas_call x0 -> x1, Pallas kernels: none -> 55.1 us  [shards(): pl.pallas_call(kernel, out_shape=(jax.ShapeDtypeStruct((PTS, 3), F32), ja...]
    reduce_sum x6 -> x0, other arithmetic: 17.4 us -> none  [the longest x2 7.98 us: kernels(): right_sq = jnp.sum(jnp.square(right.astype(jnp.float32)), axis=1)]
    dot_general x4 -> x0, matrix products: 6.2 us -> none  [kernels(): products = jnp.dot(left, right.T, preferred_element_type=jnp.float32)]
  transfers between devices with their start and end apart: 2 -> 0, of which waited for: 2 -> 0; matrix products, arithmetic and copies ran while one was open for 1% -> 0% of each run, Pallas kernels for 0% -> 0%
where the time goes in v1:
time: 59.1 us; the launch traced here: 58.9 us
  Pallas kernels  55.1 us (93%)
  local copies, waits for them, and re-layouts  3.22 us (5%)
  between operations  0.65 us (1%)
    pallas_call x1, Pallas kernels, shards(): pl.pallas_call(kernel, out_shape=(jax.ShapeDtypeStruct((PTS, 3), F32), ja...  55.1 us
    unnamed x10, local copies, waits for them, and re-layouts  3.22 us

profile of v1, /device:TPU:1, one launch (start us, length us, event | category | flops | bytes accessed | tf_op | source)
XLA Modules:
  0.0 58.9 jit_solution(17894966227064238855)
XLA Ops:
  0.6 55.1 %mmd_hsic.1 = (f32[32,3]{1,0:T(8,128)}, f32[32,3]{1,0:T(8,128)}, f32[1,3]{1,0:T(1,128)}, f32[1,3]{1,0:T(1,128)}) custom-call(bf16[32,128]{1,0:T(8,128)(2,1)} %x_hbm.1, bf16[32,128]{1,0:T(8,128)(2,1)} %y_hbm.1), custom_call_target="tpu_custom_call" | custom-call | tf_op jit(solution)/shard_map/mmd_hsic/pallas_call | solution.py:240
  55.7 0.0 copy-start
  55.7 1.4 %copy.6 = f32[32,3]{0,1:T(4,128)} copy(f32[32,3]{1,0:T(8,128)} %get-tuple-element.12) | data formatting | bytes 768
  57.1 0.0 copy-done
  57.1 0.0 copy-start.2
  57.1 0.7 %copy.7 = f32[32,3]{0,1:T(4,128)} copy(f32[32,3]{1,0:T(8,128)S(1)} %copy-done) | data formatting | bytes 768
  57.8 0.0 copy-done.2
  57.8 0.0 copy-start.1
  57.8 0.5 copy.10
  58.3 0.2 copy-done.1
  58.4 0.5 copy.11
Async XLA Ops:
  55.7 1.4 %copy-start = (f32[32,3]{1,0:T(8,128)S(1)}, f32[32,3]{1,0:T(8,128)}, u32[]{:S(2)}) copy-start(f32[32,3]{1,0:T(8,128)} %get-tuple-element.13) | copy-start | bytes 1156
  57.1 0.7 %copy-start.2 = (f32[1,3]{1,0:T(1,128)S(1)}, f32[1,3]{1,0:T(1,128)}, u32[]{:S(2)}) copy-start(f32[1,3]{1,0:T(1,128)} %get-tuple-element.10) | copy-start | bytes 40
  57.8 0.7 %copy-start.1 = (f32[1,3]{1,0:T(1,128)S(1)}, f32[1,3]{1,0:T(1,128)}, u32[]{:S(2)}) copy-start(f32[1,3]{1,0:T(1,128)} %get-tuple-element.11) | copy-start | bytes 40

commit v2 on v1

v2 whole, which is shorter than its diff:
```python
import functools
import math

import jax
import jax.numpy as jnp
from jax import lax
from jax.experimental import pallas as pl
from jax.experimental.pallas import tpu as pltpu
from jax.sharding import PartitionSpec as P

MESH = pl.DeviceIdType.MESH
NX, NZ, NY, NC = 4, 16, 4, 2
PLANE = NX * NY * NC
PTS = 32
STRIDE = 4
DIM = 128
TILES = PLANE * PTS // 128
SCALE = math.log2(math.e) / (2.0 * 0.32 * DIM)
NT = (((1,), (1,)), ((), ()))
F32 = jnp.float32
BF16 = jnp.bfloat16


def device_of(x, z, y, c):
    return ((x * NZ + z) * NY + y) * NC + c


def squares(points):
    wide = points.astype(F32)
    sq = wide * wide
    high = sq.astype(BF16)
    low = (sq - high.astype(F32)).astype(BF16)
    return high, low


def fold(tile):
    return jnp.sum(tile.reshape(-1, 8, 128), axis=0)


def powers(e):
    e2 = e * e
    return e2 * e2, e2, e


def kernel(x_hbm, y_hbm, xs_ref, ys_ref, mmd_ref, hsic_ref,
           zbuf, pbuf, rown, coln, acc, sbuf, rbuf, tsend, trecv, usend, urecv,
           load_sem, zsend_sem, zrecv_sem, psend_sem, precv_sem, dsend_sem, drecv_sem, ssend_sem, srecv_sem,
           tsend_sem, trecv_sem, usend_sem, urecv_sem):
    me = lax.axis_index("blk")
    c = lax.rem(me, NC)
    y = lax.rem(me // NC, NY)
    z = lax.rem(me // (NC * NY), NZ)
    x = me // (NC * NY * NZ)
    chip = x * NY + y
    q = c * (NX * NY) + chip

    loads = []
    for n, buf in enumerate((zbuf.at[0], pbuf.at[q])):
        for k, src in enumerate((x_hbm, y_hbm)):
            cp = pltpu.make_async_copy(src, buf.at[pl.ds(PTS * k, PTS)], load_sem.at[2 * n + k])
            cp.start()
            loads.append(cp)

    def z_peer(off):
        return (device_of(x, lax.rem(z + (off + NZ), NZ), y, c),)

    def plane_peer(dx, dy, dc):
        px, py, pc = lax.rem(x + dx, NX), lax.rem(y + dy, NY), lax.rem(c + dc, NC)
        return (device_of(px, z, py, pc),), pc * (NX * NY) + px * NY + py

    def far(v):
        return min(v, 4 - v)

    moves = sorted(((dx, dy) for dx in range(NX) for dy in range(NY) if dx or dy), key=lambda m: -far(m[0]) - far(m[1]))
    whole = [(dx, dy, dc) for dx, dy in moves for dc in (1, 0)] + [(0, 0, 1)]
    near = [sign * d for d in range(STRIDE, 0, -1) for sign in (1, -1)]

    barrier = pltpu.get_barrier_semaphore()
    for off in near:
        pl.semaphore_signal(barrier, inc=1, device_id=z_peer(off), device_id_type=MESH)
    for dx, dy in moves:
        pl.semaphore_signal(barrier, inc=1, device_id=plane_peer(dx, dy, 0)[0], device_id_type=MESH)
    pl.semaphore_signal(barrier, inc=1, device_id=plane_peer(0, 0, 1)[0], device_id_type=MESH)
    for cp in loads:
        cp.wait()
    pl.semaphore_wait(barrier, len(near) + len(moves) + 1)

    def slot_of(off):
        return 2 * off - 1 if off > 0 else -2 * off

    def send(src, dst, send_sem, recv_sem, peer):
        pltpu.make_async_remote_copy(
            src_ref=src, dst_ref=dst, send_sem=send_sem, recv_sem=recv_sem, device_id=peer, device_id_type=MESH).start()

    def send_z(source, step):
        to = slot_of(source + step)
        send(zbuf.at[slot_of(source) if source else 0], zbuf.at[to], zsend_sem, zrecv_sem.at[to], z_peer(step))

    for off in near:
        send_z(0, off)
    for dx, dy in moves:
        peer, _ = plane_peer(dx, dy, 0)
        send(zbuf.at[0], pbuf.at[q], psend_sem, precv_sem, peer)

    def wait_bytes(ref, sem):
        pltpu.make_async_copy(ref, ref, sem).wait()

    for hub in range(STRIDE, NZ // 2, STRIDE):
        for sign in (1, -1):
            at = slot_of(sign * hub)
            wait_bytes(zbuf.at[at], zrecv_sem.at[at])
            for step in range(min(STRIDE, NZ // 2 - hub - (sign < 0)), 0, -1):
                send_z(sign * hub, sign * step)
    hubs = [slot_of(sign * hub) for hub in range(STRIDE, NZ // 2, STRIDE) for sign in (1, -1)]

    wait_bytes(pbuf.at[pl.ds(0, NX * NY - 1)], precv_sem)
    half = pbuf.at[pl.ds(c * (NX * NY), NX * NY)]
    send(half, half, dsend_sem, drecv_sem, plane_peer(0, 0, 1)[0])

    acc[...] = jnp.zeros_like(acc)
    ones8 = jnp.ones((8, DIM), BF16)

    wait_bytes(half, drecv_sem)
    for g in range(TILES):
        for k in range(2):
            pts = pbuf[4 * g:4 * g + 4, PTS * k:PTS * k + PTS, :].reshape(128, DIM)
            high, low = squares(pts)
            norm = lax.dot_general(ones8, high, NT, preferred_element_type=F32)
            norm += lax.dot_general(ones8, low, NT, preferred_element_type=F32)
            rown[g, k] = norm * -SCALE

    def chunk(n, carry):
        for j in range(4):
            at = 4 * n + j
            ready = at == 0
            for hub in hubs:
                ready |= at == hub

            @pl.when(jnp.logical_not(ready))
            def _():
                wait_bytes(zbuf.at[at], zrecv_sem.at[at])

        cols = []
        for k in range(2):
            pts = zbuf[pl.ds(4 * n, 4), PTS * k:PTS * k + PTS, :].reshape(128, DIM)
            high, low = squares(pts)
            ones = jnp.ones((DIM, 128), BF16)
            norm = jnp.dot(high, ones, preferred_element_type=F32) + jnp.dot(low, ones, preferred_element_type=F32)
            coln[k] = norm * -SCALE
            cols.append(pts)
        cols = jnp.concatenate(cols, axis=0)
        own = jnp.where(n == 0, q * PTS, -PLANE * PTS)
        lane = lax.broadcasted_iota(jnp.int32, (PTS, 128), 1)
        sub = lax.broadcasted_iota(jnp.int32, (PTS, 128), 0) + own
        for g in range(TILES):
            rows_x = pbuf[4 * g:4 * g + 4, 0:PTS, :].reshape(128, DIM)
            rows_y = pbuf[4 * g:4 * g + 4, PTS:2 * PTS, :].reshape(128, DIM)
            prod_x = lax.dot_general(cols, rows_x, NT, preferred_element_type=F32)
            prod_y = lax.dot_general(cols, rows_y, NT, preferred_element_type=F32)
            part = [acc[g, i] for i in range(15)]
            for j in range(4):
                def gauss(prod, k, row):
                    arg = prod[128 * k + PTS * j:128 * k + PTS * j + PTS] * (2.0 * SCALE) + coln[k, PTS * j:PTS * j + PTS]
                    arg = (arg.reshape(-1, 8, 128) + rown[g, row][None]).reshape(PTS, 128)
                    return powers(jnp.exp2(jnp.minimum(arg, 0.0)))

                xx = gauss(prod_x, 0, 0)
                xy = gauss(prod_x, 1, 0)
                yx = gauss(prod_y, 0, 1)
                yy = gauss(prod_y, 1, 1)
                hh = [a * b for a, b in zip(xx, yy)]
                if j == 0:
                    off = lane + 128 * g != sub
                    xx = [jnp.where(off, a, 0.0) for a in xx]
                    yy = [jnp.where(off, a, 0.0) for a in yy]
                for t, stat in enumerate((xx, yy, xy, yx, hh)):
                    for b in range(3):
                        part[t * 3 + b] += fold(stat[b])
            for i in range(15):
                acc[g, i] = part[i]
        return carry

    lax.fori_loop(0, NZ // 4, chunk, 0)

    for g in range(TILES):
        def row(t, b):
            return jnp.sum(acc[g, t * 3 + b], axis=0, keepdims=True)
        zero = jnp.zeros((1, 128), F32)
        groups = [jnp.concatenate([row(k, 0), row(k, 1), row(k, 2), row(4, k) if k < 3 else zero], axis=0) for k in range(4)]
        for m in range(4):
            sbuf[4 * g + m] = jnp.concatenate([groups[k][:, PTS * m:PTS * m + PTS] for k in range(4)], axis=1)

    for move in whole:
        peer, to = plane_peer(*move)
        send(sbuf.at[to], rbuf.at[q], ssend_sem, srecv_sem, peer)
    rbuf[q] = sbuf[q]
    wait_bytes(rbuf.at[pl.ds(0, PLANE - 1)], srecv_sem)
    sums = jnp.sum(rbuf[...], axis=0)
    full = sums + 1.0
    prod = full * pltpu.roll(full, 128 - PTS, 1)
    lane = lax.broadcasted_iota(jnp.int32, (4, 128), 1)
    sub = lax.broadcasted_iota(jnp.int32, (4, 128), 0)
    packed = jnp.zeros((4, 128), F32)
    for k in range(5):
        src = prod if k == 4 else sums
        lo = PTS * (k % 4)
        tot = jnp.sum(jnp.where((lane >= lo) & (lane < lo + PTS), src, 0.0), axis=1, keepdims=True)
        packed = jnp.where(lane == 8 * sub + k, tot, packed)
    tsend[...] = jnp.sum(packed, axis=0, keepdims=True)

    for move in whole:
        send(tsend, trecv.at[q], tsend_sem, trecv_sem, plane_peer(*move)[0])
    trecv[q] = tsend[...]

    logs = jnp.log(sums)
    score = logs - pltpu.roll(logs, 64, 1)
    xs_ref[...] = score[0:3, 0:PTS]
    ys_ref[...] = score[0:3, PTS:2 * PTS]

    wait_bytes(trecv.at[pl.ds(0, PLANE - 1)], trecv_sem)
    usend[...] = jnp.sum(trecv[...], axis=0)
    for off in [NZ // 2] + [sign * d for d in range(NZ // 2 - 1, 0, -1) for sign in (1, -1)]:
        send(usend, urecv.at[z], usend_sem, urecv_sem, z_peer(off))
    urecv[z] = usend[...]
    wait_bytes(urecv.at[pl.ds(0, NZ - 1)], urecv_sem)
    tot = jnp.sum(urecv[...], axis=0)

    n = float(PTS * PLANE * NZ)

    def at(k, b):
        return tot[0:1, 8 * b + k:8 * b + k + 1]

    for b in range(3):
        txx, tyy, txy, tpr = at(0, b), at(1, b), at(2, b), at(4, b)
        th = tot[0:1, 8 * 3 + b:8 * 3 + b + 1]
        mmd_ref[0:1, b:b + 1] = n * ((txx + tyy) / (n * (n - 1.0)) - 2.0 * txy / (n * n))
        hsic_ref[0:1, b:b + 1] = (th - 2.0 * tpr / n + (txx + n) * (tyy + n) / (n * n)) / n

    wait_bytes(zbuf.at[pl.ds(0, NZ - 1)], zsend_sem)
    wait_bytes(pbuf.at[pl.ds(0, NX * NY - 1)], psend_sem)
    wait_bytes(half, dsend_sem)
    wait_bytes(sbuf.at[pl.ds(0, PLANE - 1)], ssend_sem)
    wait_bytes(trecv.at[pl.ds(0, PLANE - 1)], tsend_sem)
    wait_bytes(urecv.at[pl.ds(0, NZ - 1)], usend_sem)


def shards(x_points, y_points):
    dma = pltpu.SemaphoreType.DMA
    vmem = pl.BlockSpec(memory_space=pltpu.VMEM)
    xs, ys, mmd, hsic = pl.pallas_call(
        kernel,
        out_shape=(
            jax.ShapeDtypeStruct((3, PTS), F32),
            jax.ShapeDtypeStruct((3, PTS), F32),
            jax.ShapeDtypeStruct((1, 3), F32),
            jax.ShapeDtypeStruct((1, 3), F32),
        ),
        in_specs=[pl.BlockSpec(memory_space=pl.ANY)] * 2,
        out_specs=(vmem,) * 4,
        scratch_shapes=[
            pltpu.VMEM((NZ, 2 * PTS, DIM), BF16),
            pltpu.VMEM((PLANE, 2 * PTS, DIM), BF16),
            pltpu.VMEM((TILES, 2, 8, 128), F32),
            pltpu.VMEM((2, 128, 128), F32),
            pltpu.VMEM((TILES, 15, 8, 128), F32),
            pltpu.VMEM((PLANE, 4, 128), F32),
            pltpu.VMEM((PLANE, 4, 128), F32),
            pltpu.VMEM((1, 128), F32),
            pltpu.VMEM((PLANE, 1, 128), F32),
            pltpu.VMEM((1, 128), F32),
            pltpu.VMEM((NZ, 1, 128), F32),
            dma((4,)), dma, dma((NZ,)), dma, dma, dma, dma, dma, dma, dma, dma, dma, dma,
        ],
        compiler_params=pltpu.CompilerParams(collective_id=0, has_side_effects=True),
        name="mmd_hsic",
    )(x_points, y_points)
    return xs.T, ys.T, mmd.reshape(3), hsic.reshape(3)


def solution(mesh):
    return jax.shard_map(
        shards,
        mesh=mesh,
        in_specs=(P("blk", None), P("blk", None)),
        out_specs=(P("blk", None), P("blk", None), P(), P()),
        check_vma=False,
    )
```

time: 59.1 us -> 48.2 us (0.82)
  Pallas kernels: 55.1 us -> 44.1 us
    pallas_call x1, Pallas kernels: 55.1 us -> 44.1 us  [shards(): pl.pallas_call(kernel, out_shape=(jax.ShapeDtypeStruct((3, PTS), F32), ja...]
    unnamed x10 -> x12, local copies, waits for them, and re-layouts: 3.22 us -> 3.13 us
where the time goes in v2:
time: 48.2 us; the launch traced here: 47.9 us
  Pallas kernels  44.1 us (91%)
  local copies, waits for them, and re-layouts  3.13 us (6%)
  between operations  0.65 us (1%)
    pallas_call x1, Pallas kernels, shards(): pl.pallas_call(kernel, out_shape=(jax.ShapeDtypeStruct((3, PTS), F32), ja...  44.1 us
    unnamed x12, local copies, waits for them, and re-layouts  3.13 us

profile of v2, /device:TPU:1, one launch (start us, length us, event | category | flops | bytes accessed | tf_op | source)
XLA Modules:
  0.0 47.9 jit_solution(17351402317364901884)
XLA Ops:
  0.6 44.1 %mmd_hsic.1 = (f32[3,32]{1,0:T(4,128)}, f32[3,32]{1,0:T(4,128)}, f32[1,3]{1,0:T(1,128)}, f32[1,3]{1,0:T(1,128)}) custom-call(bf16[32,128]{1,0:T(8,128)(2,1)} %x_hbm.1, bf16[32,128]{1,0:T(8,128)(2,1)} %y_hbm.1), custom_call_target="tpu_custom_call" | custom-call | tf_op jit(solution)/shard_map/mmd_hsic/pallas_call | solution.py:250
  44.8 0.0 copy-start.1
  44.8 0.7 %copy-done.1 = f32[3,32]{1,0:T(4,128)S(1)} copy-done((f32[3,32]{1,0:T(4,128)S(1)}, f32[3,32]{1,0:T(4,128)}, u32[]{:S(2)}) %copy-start.1) | copy-done | bytes 408
  45.4 0.0 copy-start
  45.5 0.6 %copy.10 = f32[32,3]{0,1:T(4,128)} copy(f32[32,3]{0,1:T(4,128)S(1)} %bitcast.5) | data formatting | bytes 768
  46.0 0.1 copy-done
  46.1 0.0 copy-start.3
  46.1 0.6 %copy.11 = f32[32,3]{0,1:T(4,128)} copy(f32[32,3]{0,1:T(4,128)S(1)} %bitcast.4) | data formatting | bytes 768
  46.7 0.1 copy-done.3
  46.8 0.0 copy-start.2
  46.8 0.5 %copy.12 = f32[3]{0:T(128)} copy(f32[3]{0:T(128)S(1)} %bitcast.7) | data formatting | bytes 24
  47.3 0.1 copy-done.2
  47.4 0.5 %copy.13 = f32[3]{0:T(128)} copy(f32[3]{0:T(128)S(1)} %bitcast.6) | data formatting | bytes 24
Async XLA Ops:
  44.8 0.7 %copy-start.1 = (f32[3,32]{1,0:T(4,128)S(1)}, f32[3,32]{1,0:T(4,128)}, u32[]{:S(2)}) copy-start(f32[3,32]{1,0:T(4,128)} %get-tuple-element.8) | copy-start | bytes 1156
  45.4 0.7 %copy-start = (f32[3,32]{1,0:T(4,128)S(1)}, f32[3,32]{1,0:T(4,128)}, u32[]{:S(2)}) copy-start(f32[3,32]{1,0:T(4,128)} %get-tuple-element.9) | copy-start | bytes 1156
  46.1 0.7 %copy-start.3 = (f32[1,3]{1,0:T(1,128)S(1)}, f32[1,3]{1,0:T(1,128)}, u32[]{:S(2)}) copy-start(f32[1,3]{1,0:T(1,128)} %get-tuple-element.10) | copy-start | bytes 40
  46.8 0.6 %copy-start.2 = (f32[1,3]{1,0:T(1,128)S(1)}, f32[1,3]{1,0:T(1,128)}, u32[]{:S(2)}) copy-start(f32[1,3]{1,0:T(1,128)} %get-tuple-element.11) | copy-start | bytes 40
